TPU v7x, 32 devices: a whole 2x2x4 slice. The times are simulated.
32 devices in a mesh: ens: 2 (over y), space: 4 (over z), chan: 2 (over x), sub: 2 (over core).
Axes of the slice: x: 2, y: 2, z: 4, core: 2. Of those that a mesh axis runs over, the one named last changes fastest.
Arguments:
- node_state: bfloat16 [8192, 512], P(('ens', 'space'), ('chan', 'sub')), parts along dimension 0, may hold values from -6 to 6
- norm_gains: float32 [2, 512], replicated, may hold values from 0.25 to 1.75
- norm_shifts: float32 [2, 512], replicated, may hold values from -3 to 3
- query_weight: bfloat16 [512, 512], P(None, 'chan')
- key_weight: bfloat16 [512, 512], P(None, 'chan')
- value_weight: bfloat16 [512, 512], P(None, 'chan'), may hold values from -0.25 to 0.25
- out_weight: bfloat16 [512, 512], replicated, may hold values from -0.25 to 0.25
- ffn_in: bfloat16 [2048, 512], P('chan'), may hold values from -0.25 to 0.25
- ffn_out: bfloat16 [2048, 512], P('chan'), may hold values from -0.125 to 0.125
- live_counts: int32 [4], P('space'), may hold values from 512 to 1024, as said below
- send_rows: int32 [4, 2, 256], P('space'), may hold values from 0 to 1023, as said below
- tile_keys: int32 [32, 12], P('space'), may hold values from 0 to 11, as said below
- tile_bits: int32 [32, 12, 4, 128], P('space'), may hold values from -2147483648 to 2147483647, as said below
Outputs:
- updated: bfloat16 [8192, 512], P(('ens', 'space'), ('chan', 'sub')), parts along dimension 0
There are 2 independent parts, one for each index of `ens`. A program takes and returns all parts, laid end to end along the dimension named above; an argument that names none is the same for every part. Nothing has to cross between parts.
Inputs may be any that keep to these rules, and one draw needn't show every extreme that they name: Partition s has live nodes 0 to live_counts[s] - 1; the first and the last partition are full. send_rows[s, 0] lists nodes of partition s read by its lower neighbour, send_rows[s, 1] those read by its upper neighbour; all are live nodes, and entries may repeat. `tile_keys`: slot 0 of every block names the block itself (its index within the partition); other slots name blocks of the same partition (below 8), of the lower halo (from 8) or of the upper halo (from 10); the first partition names no lower halo and the last no upper halo. `tile_bits`: bit j of word w in column r of a slot says whether query r of the block may attend key 32 w + j of the slot's block (bit 31 is the sign bit); in slot 0 every query's own bit is set. Slots whose words are all zero carry no edges.
All inputs are finite; a program needn't handle non-finite values.
Results may differ from a plain program's by a relative error of at most 0.0095.
Values may be sent and summed in bfloat16 or wider, within the bound.
A program may use at most 64 MiB of HBM per device.

v0:
```python
import math

import jax
import jax.numpy as jnp
from jax import lax
from jax.sharding import PartitionSpec as P

HD = 64


NORM_EPS = 1e-05
NEG_FILL = -1e30


def padded_2(array, sides, width):
    for axis, dim in sides:
        size, length = (lax.axis_size(axis), array.shape[dim])
        up = [(i, (i + 1) % size) for i in range(size - 1)]
        down = [(j, i) for i, j in up]
        last = lax.slice_in_dim(array, length - width, length, axis=dim)
        leading = lax.slice_in_dim(array, 0, width, axis=dim)
        before = lax.ppermute(last, axis, up)
        after = lax.ppermute(leading, axis, down)
        array = jnp.concatenate([before, array, after], axis=dim)
    return array


def normalize_rows(source, gain_row, shift_row):
    row_mean = jnp.mean(source, axis=-1, keepdims=True)
    spread = jnp.mean(source * source, axis=-1, keepdims=True) - row_mean * row_mean
    return (source - row_mean) * lax.rsqrt(spread + NORM_EPS) * gain_row + shift_row


def unpack_allowed(key_bits, key_ids, live_count, tile_size, blocks_own):
    shifts = jnp.arange(32, dtype=jnp.int32)
    expanded = jnp.right_shift(key_bits[..., None, :], shifts[:, None]) & 1
    lead_shape = key_bits.shape[:-2]
    expanded = expanded.reshape(lead_shape + (tile_size, tile_size))
    key_index = key_ids[..., None] * tile_size + jnp.arange(tile_size, dtype=jnp.int32)
    key_live = (key_ids[..., None] >= blocks_own) | (key_index < live_count)
    slot_count = key_ids.shape[-1]
    slot_first = jnp.arange(slot_count, dtype=jnp.int32)[:, None, None] == 0
    diagonal = (
        jnp.arange(tile_size, dtype=jnp.int32)[:, None]
        == jnp.arange(tile_size, dtype=jnp.int32)[None, :]
    )
    own_bit = slot_first & diagonal[None]
    return (expanded == 1) & (key_live[..., None] | own_bit)


def hidden_term(rows, in_piece, out_piece):
    hidden = jax.nn.gelu(
        lax.dot_general(
            rows, in_piece, (((1,), (1,)), ((), ())), preferred_element_type=jnp.float32
        )
    ).astype(jnp.bfloat16)
    return jnp.dot(hidden, out_piece, preferred_element_type=jnp.float32)


def on_device(
    node_state,
    norm_gains,
    norm_shifts,
    query_weight,
    key_weight,
    value_weight,
    out_weight,
    ffn_in,
    ffn_out,
    live_counts,
    send_rows,
    tile_keys,
    tile_bits,
):
    n_chan = lax.axis_size("chan")
    n_sub = lax.axis_size("sub")
    groups = n_chan * n_sub
    chan_at = lax.axis_index("chan")
    sub_at = lax.axis_index("sub")
    node_rank = chan_at * n_sub + sub_at
    node_count = node_state.shape[0]
    tile_size = tile_bits.shape[-1]
    word_count = tile_bits.shape[-2]
    slot_count = tile_keys.shape[1]
    blocks_own = tile_keys.shape[0]
    per_rank = node_count // groups
    head_cols = query_weight.shape[1]
    heads_here = head_cols // HD
    halo_rows = send_rows.shape[-1]
    live_count = live_counts[0]

    def own_half(source):
        step_rows = source.shape[0] // groups
        shaped = source.reshape((n_chan, n_sub, step_rows) + source.shape[1:])
        picked = lax.dynamic_index_in_dim(shaped, sub_at, 1, keepdims=False)
        return picked.reshape((n_chan * step_rows,) + source.shape[1:])

    node_rows = lax.all_to_all(node_state, ("chan", "sub"), split_axis=0, concat_axis=1, tiled=True)
    pair_weight = jnp.concatenate([key_weight, value_weight], axis=1)
    gathered = lax.all_gather(node_state, ("chan", "sub"), axis=1, tiled=True)
    normed = normalize_rows(gathered.astype(jnp.float32), norm_gains[0], norm_shifts[0]).astype(
        jnp.bfloat16
    )
    key_values = jnp.dot(normed, pair_weight, preferred_element_type=jnp.float32).astype(
        jnp.bfloat16
    )
    queries = jnp.dot(own_half(normed), query_weight, preferred_element_type=jnp.float32).astype(
        jnp.bfloat16
    )
    send_list = send_rows.reshape(2 * halo_rows)
    outgoing = jnp.take(key_values, send_list, axis=0)
    padded = padded_2(outgoing, (("space", 0),), halo_rows)
    extended = jnp.concatenate([key_values, padded[:halo_rows], padded[-halo_rows:]], axis=0)
    key_blocks = extended.reshape(-1, tile_size, 2 * head_cols)
    key_ids = own_half(tile_keys)
    key_bits = own_half(tile_bits)
    block_total = key_ids.shape[0]
    per_round = math.gcd(block_total, 4)
    rounds = block_total // per_round
    score_scale = 1.0 / math.sqrt(HD)

    def attend(inputs):
        q_part, id_part, bit_part = inputs
        chosen = key_blocks[id_part]
        keys_part = chosen[..., :head_cols].reshape(
            per_round, slot_count, tile_size, heads_here, HD
        )
        values_part = chosen[..., head_cols:].reshape(
            per_round, slot_count, tile_size, heads_here, HD
        )
        scores = (
            jnp.einsum("grhd,gtkhd->ghrtk", q_part, keys_part, preferred_element_type=jnp.float32)
            * score_scale
        )
        allowed = unpack_allowed(bit_part, id_part, live_count, tile_size, blocks_own)
        allowed = jnp.transpose(allowed, (0, 3, 1, 2))[:, None]
        masked = jnp.where(allowed, scores, NEG_FILL)
        row_max = jnp.max(masked, axis=(3, 4), keepdims=True)
        weights = jnp.where(allowed, jnp.exp(scores - row_max), 0.0)
        row_total = jnp.sum(weights, axis=(3, 4))
        mixed_heads = jnp.einsum(
            "ghrtk,gtkhd->grhd",
            weights.astype(jnp.bfloat16),
            values_part,
            preferred_element_type=jnp.float32,
        )
        mixed_heads = mixed_heads / jnp.transpose(row_total, (0, 2, 1))[..., None]
        return mixed_heads.astype(jnp.bfloat16).reshape(per_round * tile_size, head_cols)

    query_groups = queries.reshape(rounds, per_round, tile_size, heads_here, HD)
    attended = lax.map(
        attend,
        (
            query_groups,
            key_ids.reshape(rounds, per_round, slot_count),
            key_bits.reshape(rounds, per_round, slot_count, word_count, tile_size),
        ),
    )
    mixed_rows = jnp.dot(
        lax.all_to_all(
            attended.reshape(n_chan, per_rank, head_cols),
            "chan",
            split_axis=0,
            concat_axis=2,
            tiled=True,
        )[0],
        out_weight,
        preferred_element_type=jnp.float32,
    )
    after_attn = node_rows.astype(jnp.float32) + mixed_rows
    normed_two = normalize_rows(after_attn, norm_gains[1], norm_shifts[1]).astype(jnp.bfloat16)
    all_rows = lax.all_gather(normed_two, "chan", axis=0, tiled=True)
    update = lax.psum_scatter(
        hidden_term(all_rows, ffn_in, ffn_out).astype(jnp.bfloat16),
        "chan",
        scatter_dimension=0,
        tiled=True,
    ).astype(jnp.float32)
    position = node_rank * per_rank + jnp.arange(per_rank, dtype=jnp.int32)
    result = jnp.where((position < live_count)[:, None], after_attn + update, 0.0).astype(
        jnp.bfloat16
    )
    return lax.all_to_all(result, ("chan", "sub"), split_axis=1, concat_axis=0, tiled=True)


def solution(mesh):
    in_specs = (
        P(("ens", "space"), ("chan", "sub")),
        P(),
        P(),
        P(None, "chan"),
        P(None, "chan"),
        P(None, "chan"),
        P(),
        P("chan", None),
        P("chan", None),
        P("space"),
        P("space", None, None),
        P("space", None),
        P("space", None, None, None),
    )
    out_specs = P(("ens", "space"), ("chan", "sub"))
    return jax.shard_map(
        on_device, mesh=mesh, in_specs=in_specs, out_specs=out_specs, check_vma=False
    )
```

profile of v0, /device:TPU:0, one launch (start us, length us, event | category | flops | bytes accessed | tf_op | source)
XLA Modules:
  0.0 127.2 jit_solution(3869248447497856356)
XLA Ops:
  7.3 4.2 %all-to-all-start = ((bf16[4,256,128]{2,1,0:T(8,128)(2,1)}), bf16[4,256,128]{2,1,0:T(8,128)(2,1)}, u32[]{:S(2)}, u32[]{:S(2)}) async-start(bf16[4,256,128]{2,1,0:T(8,128)(2,1)} %bitcast.86), calls=%async_computation | async-start | bytes 524288 | tf_op jit(solution)/shard_map/all_to_all | solution.py:98
  15.6 1.2 fusion.10
  18.5 10.0 %all-gather.2.cloned.1.call-done = bf16[1024,512]{1,0:T(8,128)(2,1)} async-done(((bf16[1024,128]{1,0:T(8,128)(2,1)}), bf16[1024,512]{1,0:T(8,128)(2,1)}) %all-gather.2.cloned.1.call-update) | async-done | bytes 1048592 | tf_op jit(solution)/shard_map/all_gather | solution.py:100
  28.5 1.6 %convert_reduce_fusion = (f32[1024]{0:T(1024)S(1)}, f32[1024]{0:T(1024)S(1)}) fusion(bf16[1024,512]{1,0:T(8,128)(2,1)} %all-gather.2.cloned.1.call-done), kind=kLoop, calls=%fused_computation.17 | loop fusion | flops 2095104 | bytes 1056768 | tf_op jit(solution)/shard_map/reduce_sum | solution.py:29
  30.1 1.7 %fusion.14 = bf16[1024,512]{1,0:T(8,128)(2,1)S(1)} fusion(bf16[1024,512]{1,0:T(8,128)(2,1)} %all-gather.2.cloned.1.call-done, f32[512]{0:T(512)S(1)} %bitcast.103, f32[512]{0:T(512)S(1)} %bitcast.102, f32[1024]{0:T(1024)S(1)} %get-tuple-element.41, f32[1024]{0:T(1024)S(1)} %get-tuple-element.40), kind=kLoop, calls=%fused_computation.22 | loop fusion | flops 3145728 | bytes 2109440 | tf_op jit(solution)/shard_map/convert_element_type | solution.py:101
  33.5 2.0 %gather_fusion = bf16[512,512]{1,0:T(8,128)(2,1)S(1)} fusion(bf16[1024,512]{1,0:T(8,128)(2,1)S(1)} %convolution_convert_fusion, s32[1024]{0:T(1024)S(1)} %pad_clamp_fusion.1), kind=kCustom, calls=%fused_computation | custom fusion | bytes 1050624 | tf_op jit(solution)/shard_map/jit(_take)/gather | solution.py:111
  35.7 3.4 %collective-permute-start = (bf16[256,512]{1,0:T(8,128)(2,1)S(1)}, bf16[256,512]{1,0:T(8,128)(2,1)S(1)}, u32[]{:S(2)}, u32[]{:S(2)}) collective-permute-start(bf16[256,512]{1,0:T(8,128)(2,1)S(1)} %get-tuple-element.34), channel_id=1, source_target_pairs={{0,4},{4,8},{8,12},{1,5},{5,9},{9,13},{2,6},{6,10},{10,14},{3,7},{... | collective-permute-start | bytes 786440 | tf_op jit(solution)/shard_map/ppermute | solution.py:22
  39.1 1.3 %collective-permute-start.1 = (bf16[256,512]{1,0:T(8,128)(2,1)S(1)}, bf16[256,512]{1,0:T(8,128)(2,1)}, u32[]{:S(2)}, u32[]{:S(2)}) collective-permute-start(bf16[256,512]{1,0:T(8,128)(2,1)S(1)} %get-tuple-element.35), channel_id=1, source_target_pairs={{4,0},{8,4},{12,8},{5,1},{9,5},{13,9},{6,2},{10,6},{14,10},{7,3},{... | collective-permute-start | bytes 786440 | tf_op jit(solution)/shard_map/ppermute | solution.py:23
  40.4 1.1 constant_dynamic-slice_fusion
  42.9 2.2 %collective-permute-done = bf16[256,512]{1,0:T(8,128)(2,1)S(1)} collective-permute-done((bf16[256,512]{1,0:T(8,128)(2,1)S(1)}, bf16[256,512]{1,0:T(8,128)(2,1)S(1)}, u32[]{:S(2)}, u32[]{:S(2)}) %collective-permute-start) | collective-permute-done | bytes 262176 | tf_op jit(solution)/shard_map/ppermute | solution.py:22
  45.7 3.5 %collective-permute-done.1 = bf16[256,512]{1,0:T(8,128)(2,1)} collective-permute-done((bf16[256,512]{1,0:T(8,128)(2,1)S(1)}, bf16[256,512]{1,0:T(8,128)(2,1)}, u32[]{:S(2)}, u32[]{:S(2)}) %collective-permute-start.1) | collective-permute-done | bytes 262176 | tf_op jit(solution)/shard_map/ppermute | solution.py:23
  49.3 1.5 %pad_maximum_fusion = bf16[1536,512]{1,0:T(8,128)(2,1)S(1)} fusion(bf16[256,512]{1,0:T(8,128)(2,1)} %collective-permute-done.1, bf16[256,512]{1,0:T(8,128)(2,1)} %copy-done.5, bf16[1024,512]{1,0:T(8,128)(2,1)} %copy-done.1), kind=kLoop, calls=%fused_computation.32 | loop fusion | flops 4718592 | bytes 3145728 | tf_op jit(solution)/shard_map/concatenate | solution.py:113
  50.8 5.0 %gather_fusion.1 = bf16[48,128,512]{2,1,0:T(8,128)(2,1)} fusion(bf16[12,128,512]{2,1,0:T(8,128)(2,1)S(1)} %bitcast.77, s32[1024]{0:T(1024)S(1)} %pad_clamp_fusion), kind=kCustom, calls=%fused_computation.1 | custom fusion | bytes 12583104 | tf_op jit(solution)/shard_map/while/body/eval_jaxpr/gather | solution.py:124
  55.7 8.6 %copy.29 = bf16[48,128,512]{1,2,0:T(8,128)(2,1)} copy(bf16[48,128,512]{2,1,0:T(8,128)(2,1)} %gather_fusion.1) | data formatting | bytes 12582912 | tf_op jit(solution)/shard_map/while/body/eval_jaxpr/gather | solution.py:124
  64.4 3.6 %fusion.57 = (bf16[4,12,128,256]{2,3,1,0:T(8,128)(2,1)S(1)}, bf16[4,12,128,256]{2,3,1,0:T(8,128)(2,1)S(1)}) fusion(bf16[4,12,128,512]{2,3,1,0:T(8,128)(2,1)} %bitcast.78), kind=kLoop, calls=%fused_computation.83 | loop fusion | bytes 12582912 | tf_op jit(solution)/shard_map/while/body/eval_jaxpr/slice | solution.py:128
  68.0 3.1 %select_reduce_fusion = (f32[4,4,128]{2,1,0:T(4,128)S(1)}, f32[4,4,128,12,128]{2,4,3,1,0:T(8,128)S(1)}) fusion(pred[4,128,12,128]{1,3,2,0:T(8,128)(4,1)S(1)} %bitcast.79, bf16[4,12,128,4,64]{2,4,3,1,0:T(8,128)(2,1)S(1)} %bitcast.83, bf16[4,128,4,64,1]{3,2,1,0,4:T(4,128)(2,1)S(1)} %bitcast.89), kind=kOutput, calls=%fused_computation.3 | convolution fusion | flops 412088320 | bytes 16785408 | tf_op jit(solution)/shard_map/while/body/eval_jaxpr/grhd,gtkhd->ghrtk/dot_general | solution.py:132
  71.2 2.8 %fusion = f32[4,4,128]{2,1,0:T(4,128)S(1)} fusion(f32[4,4,128,12,128]{2,4,3,1,0:T(8,128)S(1)} %get-tuple-element.45, f32[4,4,128]{2,1,0:T(4,128)S(1)} %get-tuple-element.44, pred[4,128,12,128]{1,3,2,0:T(8,128)(4,1)S(1)} %bitcast.80), kind=kLoop, calls=%fused_computation.4 | loop fusion | flops 12580864 | bytes 13385728 | tf_op jit(solution)/shard_map/while/body/eval_jaxpr/reduce_sum | solution.py:140
  74.0 3.4 %fusion.38 = bf16[4,128,4,64]{1,3,2,0:T(8,128)(2,1)S(1)} fusion(f32[4,4,128,12,128]{2,4,3,1,0:T(8,128)S(1)} %get-tuple-element.45, f32[4,4,128]{2,1,0:T(4,128)S(1)} %get-tuple-element.44, pred[4,128,12,128]{1,3,2,0:T(8,128)(4,1)S(1)} %bitcast.81, bf16[4,12,128,4,64]{2,4,3,1,0:T(8,128)(2,1)S(1)} %bitcast.82, f32[4,128,4]{1,2,0:T(4,128)S(1)} %bitcast.93), kind=kOutput, calls=%fused_computation.42 | convolution fusion | flops 415498240 | bytes 16793600 | tf_op jit(solution)/shard_map/while/body/eval_jaxpr/ghrtk,gtkhd->grhd/dot_general | solution.py:141
  77.8 7.6 %all_to_all.47 = bf16[2,256,256]{1,2,0:T(8,128)(2,1)S(1)} all-to-all(bf16[2,256,256]{1,2,0:T(8,128)(2,1)S(1)} %copy.36), channel_id=1, replica_groups=mesh['ens'=2,'space'=4,'chan'=2,'sub'=2] {'chan'}, dimensions={0} | all-to-all | bytes 524288 | tf_op jit(solution)/shard_map/all_to_all | solution.py:160
  85.4 1.4 %fusion.56 = (f32[256]{0:T(256)S(1)}, f32[256]{0:T(256)S(1)}, f32[256,512]{1,0:T(8,128)S(1)}) fusion(bf16[256,512]{0,1:T(8,128)(2,1)S(1)} %bitcast.88, bf16[512,512]{1,0:T(8,128)(2,1)S(1)} %copy-done.4, bf16[4,256,128]{2,1,0:T(8,128)(2,1)} %all-to-all-done), kind=kOutput, calls=%fused_computation.82 | convolution fusion | flops 134872576 | bytes 1574912 | tf_op jit(solution)/shard_map/dot_general | solution.py:159
  87.0 7.0 %all_gather.7 = bf16[512,512]{1,0:T(8,128)(2,1)S(1)} all-gather(bf16[256,512]{1,0:T(8,128)(2,1)S(1)} %add_convert_fusion), channel_id=1, replica_groups=mesh['ens'=2,'space'=4,'chan'=2,'sub'=2] {'chan'}, dimensions={0}, use_global_device_ids=true | all-gather | bytes 786432 | tf_op jit(solution)/shard_map/all_gather | solution.py:172
  94.0 2.3 %convolution_convert_fusion.1 = bf16[512,512]{1,0:T(8,128)(2,1)} fusion(bf16[1024,512]{1,0:T(8,128)(2,1)S(1)} %copy-done, bf16[512,512]{1,0:T(8,128)(2,1)S(1)} %all_gather.7, bf16[1024,512]{1,0:T(8,128)(2,1)S(1)} %copy-done.7), kind=kOutput, calls=%fused_computation.34 | convolution fusion | flops 1078722560 | bytes 3145728 | tf_op jit(solution)/shard_map/dot_general | solution.py:57
  96.3 13.8 %reduce-scatter.2.cloned.1.call-done = bf16[256,512]{1,0:T(8,128)(2,1)} async-done(((bf16[512,512]{1,0:T(8,128)(2,1)}), bf16[256,512]{1,0:T(8,128)(2,1)}) %reduce-scatter.2.cloned.1.call-update) | async-done | bytes 262160 | tf_op jit(solution)/shard_map/reduce_scatter | solution.py:173
  111.2 8.4 %all_to_all.48 = bf16[256,4,128]{2,0,1:T(8,128)(2,1)S(1)} all-to-all(bf16[256,4,128]{2,0,1:T(8,128)(2,1)S(1)} %copy_bitcast_fusion), channel_id=1, replica_groups=mesh['ens'=2,'space'=4,'chan'=2,'sub'=2] {'chan','sub'}, dimensions={1} | all-to-all | bytes 524288 | tf_op jit(solution)/shard_map/all_to_all | solution.py:183
  (59 shorter events, 12.1 us)
Async XLA Ops:
  6.5 87.5 %copy-start = (bf16[1024,512]{1,0:T(8,128)(2,1)S(1)}, bf16[1024,512]{1,0:T(8,128)(2,1)}, u32[]{:S(2)}) copy-start(bf16[1024,512]{1,0:T(8,128)(2,1)} %param.21) | copy-start | bytes 3145732
  6.5 26.2 %copy-start.9 = (bf16[512,256]{1,0:T(8,128)(2,1)S(1)}, bf16[512,256]{1,0:T(8,128)(2,1)}, u32[]{:S(2)}) copy-start(bf16[512,256]{1,0:T(8,128)(2,1)} %param.17) | copy-start | bytes 786436
  6.5 26.2 %copy-start.8 = (bf16[512,256]{1,0:T(8,128)(2,1)S(1)}, bf16[512,256]{1,0:T(8,128)(2,1)}, u32[]{:S(2)}) copy-start(bf16[512,256]{1,0:T(8,128)(2,1)} %param.18) | copy-start | bytes 786436
  6.5 21.9 %all-gather.2.cloned.1.call-start = ((), (), s32[]{:S(2)}) async-start(), calls=%async_computation.4 | async-start | bytes 1310720 | tf_op jit(solution)/shard_map/all_gather | solution.py:100
  7.3 70.6 %all-to-all-start = ((bf16[4,256,128]{2,1,0:T(8,128)(2,1)}), bf16[4,256,128]{2,1,0:T(8,128)(2,1)}, u32[]{:S(2)}, u32[]{:S(2)}) async-start(bf16[4,256,128]{2,1,0:T(8,128)(2,1)} %bitcast.86), calls=%async_computation | async-start | bytes 524288 | tf_op jit(solution)/shard_map/all_to_all | solution.py:98
  11.5 98.7 %reduce-scatter.2.cloned.1.call-start = ((), (), s32[]{:S(2)}) async-start(), calls=%async_computation.5 | async-start | bytes 786432 | tf_op jit(solution)/shard_map/reduce_scatter | solution.py:173
  31.7 1.0 copy-start.2
  33.5 2.2 %copy-start.1 = (bf16[1024,512]{1,0:T(8,128)(2,1)}, bf16[1024,512]{1,0:T(8,128)(2,1)S(1)}, u32[]{:S(2)}) copy-start(bf16[1024,512]{1,0:T(8,128)(2,1)S(1)} %convolution_convert_fusion) | copy-start | bytes 3145732
  35.5 6.0 %copy-start.6 = (bf16[512,256]{1,0:T(8,128)(2,1)S(1)}, bf16[512,256]{1,0:T(8,128)(2,1)}, u32[]{:S(2)}) copy-start(bf16[512,256]{1,0:T(8,128)(2,1)} %param.16) | copy-start | bytes 786436
  35.7 9.3 %collective-permute-start = (bf16[256,512]{1,0:T(8,128)(2,1)S(1)}, bf16[256,512]{1,0:T(8,128)(2,1)S(1)}, u32[]{:S(2)}, u32[]{:S(2)}) collective-permute-start(bf16[256,512]{1,0:T(8,128)(2,1)S(1)} %get-tuple-element.34), channel_id=1, source_target_pairs={{0,4},{4,8},{8,12},{1,5},{5,9},{9,13},{2,6},{6,10},{10,14},{3,7},{... | collective-permute-start | bytes 786440 | tf_op jit(solution)/shard_map/ppermute | solution.py:22
  39.1 10.2 %collective-permute-start.1 = (bf16[256,512]{1,0:T(8,128)(2,1)S(1)}, bf16[256,512]{1,0:T(8,128)(2,1)}, u32[]{:S(2)}, u32[]{:S(2)}) collective-permute-start(bf16[256,512]{1,0:T(8,128)(2,1)S(1)} %get-tuple-element.35), channel_id=1, source_target_pairs={{4,0},{8,4},{12,8},{5,1},{9,5},{13,9},{6,2},{10,6},{14,10},{7,3},{... | collective-permute-start | bytes 786440 | tf_op jit(solution)/shard_map/ppermute | solution.py:23
  45.0 0.7 copy-start.5
  64.4 3.6 %copy-start.3 = (bf16[4,128,4,64]{3,2,1,0:T(4,128)(2,1)S(1)}, bf16[4,128,4,64]{3,2,1,0:T(4,128)(2,1)}, u32[]{:S(2)}) copy-start(bf16[4,128,4,64]{3,2,1,0:T(4,128)(2,1)} %reshape.235) | copy-start | bytes 786436
  74.0 11.5 %copy-start.4 = (bf16[512,512]{1,0:T(8,128)(2,1)S(1)}, bf16[512,512]{1,0:T(8,128)(2,1)}, u32[]{:S(2)}) copy-start(bf16[512,512]{1,0:T(8,128)(2,1)} %param.19) | copy-start | bytes 1572868
  77.4 16.6 %copy-start.7 = (bf16[1024,512]{1,0:T(8,128)(2,1)S(1)}, bf16[1024,512]{1,0:T(8,128)(2,1)}, u32[]{:S(2)}) copy-start(bf16[1024,512]{1,0:T(8,128)(2,1)} %param.20) | copy-start | bytes 3145732
Sparse Core Ops, SparseCore 0:
  8.9 19.5 all-gather.1
  96.4 13.6 reduce-scatter.1
where the time goes:
time: 128 us; the launch traced here: 127 us
  waiting for transfers between devices  30.2 us (24%)
  local copies, waits for them, and re-layouts  28.3 us (22%)
  blocking collectives  23 us (18%)
  between operations  14.3 us (11%)
  other arithmetic  11.2 us (9%)
  matrix products  11.2 us (9%)
  starting transfers between devices  8.95 us (7%)
    reduce_scatter x1, waiting for transfers between devices, on_device(): lax.psum_scatter(hidden_term(all_rows, ffn_in, ffn_out).astype(jnp.bfloat...  13.8 us
    gather x2, local copies, waits for them, and re-layouts, attend(): chosen = key_blocks[id_part]  13.6 us
    all_gather x1, waiting for transfers between devices, on_device(): gathered = lax.all_gather(node_state, ('chan', 'sub'), axis=1, tiled=True)  10 us
    all_to_all x1, blocking collectives, on_device(): lax.all_to_all(result, ('chan', 'sub'), split_axis=1, concat_axis=0, tile...  8.39 us
    all_to_all x1, blocking collectives, on_device(): lax.all_to_all(attended.reshape(n_chan, per_rank, head_cols), 'chan', spl...  7.56 us
    all_gather x1, blocking collectives, on_device(): all_rows = lax.all_gather(normed_two, 'chan', axis=0, tiled=True)  7.04 us
    all_to_all x1, starting transfers between devices, on_device(): lax.all_to_all(node_state, ('chan', 'sub'), split_axis=0, concat_axis=1,...  4.25 us
    unnamed x23, local copies, waits for them, and re-layouts  3.83 us
  transfers between devices with their start and end apart: 5, of which 4 were waited for; matrix products, arithmetic and copies ran while one was open for 34% of the time, Pallas kernels for 0%

commit v1 on v0

--- a/solution.py
+++ b/solution.py
@@ -3,6 +3,8 @@
 import jax
 import jax.numpy as jnp
 from jax import lax
+from jax.experimental import pallas as pl
+from jax.experimental.pallas import tpu as pltpu
 from jax.sharding import PartitionSpec as P
 
 HD = 64
@@ -183,6 +185,470 @@
     return lax.all_to_all(result, ("chan", "sub"), split_axis=1, concat_axis=0, tiled=True)
 
 
+MESH = pl.DeviceIdType.MESH
+LOG2E = 1.4426950408889634
+NT = (((1,), (1,)), ((), ()))
+
+
+def gelu_tanh(u):
+    inner = 0.7978845608028654 * (u + 0.044715 * (u * u * u))
+    return 0.5 * u * (1.0 + jnp.tanh(inner))
+
+
+def layer_kernel(
+    x_ref,
+    gains_ref,
+    shifts_ref,
+    wq_hbm,
+    wk_hbm,
+    wv_hbm,
+    wo_hbm,
+    fin_hbm,
+    fout_hbm,
+    live_ref,
+    send_ref,
+    tk_ref,
+    bits_ref,
+    out_ref,
+    gx,
+    hsend,
+    nbuf,
+    kbuf,
+    vbuf,
+    wvt,
+    qbuf,
+    bias_ref,
+    att,
+    own_part,
+    psend,
+    precv,
+    osend,
+    wq,
+    wk,
+    wv,
+    wo,
+    fin,
+    fout,
+    w_sem,
+    loc_sem,
+    a_send,
+    a_recv,
+    b_send,
+    b_recv,
+    c_send,
+    c_recv,
+    z_send,
+    z_recv,
+    t_send,
+    t_recv,
+    p_send,
+    p_recv,
+    o_send,
+    o_recv,
+):
+    f32, bf16 = jnp.float32, jnp.bfloat16
+    rows, cols = x_ref.shape
+    groups, ext_rows, _ = gx.shape
+    tile = bits_ref.shape[-1]
+    words = bits_ref.shape[-2]
+    slots = tk_ref.shape[1]
+    blocks_own = tk_ref.shape[0]
+    halo = send_ref.shape[-1]
+    head_cols = wq.shape[1]
+    pairs = head_cols // (2 * HD)
+    pw = 2 * HD
+    half_rows = rows // 2
+    blocks_here = blocks_own // 2
+    chunk = 2 * tile
+    n_own = rows // chunk
+    n_halo = 2 * halo // chunk
+    per = chunk // tile
+
+    c = lax.axis_index("chan")
+    s = lax.axis_index("sub")
+    z = lax.axis_index("space")
+    nz = lax.axis_size("space")
+    own = c * 2 + s
+    xslot = (1 - c) * 2 + s
+    xdev = {"chan": 1 - c}
+    sdev = {"sub": 1 - s}
+    has_up = z < nz - 1
+    has_down = z > 0
+
+    weights = ((wk_hbm, wk), (wv_hbm, wv), (wq_hbm, wq), (wo_hbm, wo), (fin_hbm, fin), (fout_hbm, fout))
+    w_copies = [pltpu.make_async_copy(a, b, w_sem.at[i]) for i, (a, b) in enumerate(weights)]
+    for w_copy in w_copies:
+        w_copy.start()
+    local = pltpu.make_async_copy(x_ref, gx.at[own, pl.ds(0, rows)], loc_sem)
+    local.start()
+
+    barrier = pltpu.get_barrier_semaphore()
+    pl.semaphore_signal(barrier, inc=1, device_id=xdev, device_id_type=MESH)
+    pl.semaphore_signal(barrier, inc=1, device_id=sdev, device_id_type=MESH)
+
+    @pl.when(has_up)
+    def _():
+        pl.semaphore_signal(barrier, inc=1, device_id={"space": z + 1}, device_id_type=MESH)
+
+    @pl.when(has_down)
+    def _():
+        pl.semaphore_signal(barrier, inc=1, device_id={"space": z - 1}, device_id_type=MESH)
+
+    pl.semaphore_wait(barrier, 2 + jnp.where(has_up, 1, 0) + jnp.where(has_down, 1, 0))
+
+    def rdma(src, dst, ss, rs, dev):
+        return pltpu.make_async_remote_copy(
+            src_ref=src, dst_ref=dst, send_sem=ss, recv_sem=rs, device_id=dev, device_id_type=MESH
+        )
+
+    def a_copy():
+        return rdma(x_ref, gx.at[own, pl.ds(0, rows)], a_send.at[0], a_recv.at[0], sdev)
+
+    def b_copy(i):
+        at = pl.ds(i * chunk, chunk)
+        return rdma(x_ref.at[at], gx.at[own, at], b_send.at[i], b_recv.at[i], xdev)
+
+    def c_copy(i):
+        at = pl.ds(i * chunk, chunk)
+        return rdma(gx.at[xslot, at], gx.at[xslot, at], c_send.at[i], c_recv.at[i], sdev)
+
+    tail_at = pl.ds(rows, 2 * halo)
+
+    def a2_copy():
+        return rdma(gx.at[own, tail_at], gx.at[own, tail_at], a_send.at[1], a_recv.at[1], sdev)
+
+    def b2_copy():
+        return rdma(gx.at[own, tail_at], gx.at[own, tail_at], b_send.at[n_own], b_recv.at[n_own], xdev)
+
+    def c2_copy():
+        return rdma(
+            gx.at[xslot, tail_at], gx.at[xslot, tail_at], c_send.at[n_own], c_recv.at[n_own], sdev
+        )
+
+    def up_copy():
+        return rdma(
+            hsend.at[1], gx.at[own, pl.ds(rows, halo)], z_send.at[1], z_recv.at[1], {"space": z + 1}
+        )
+
+    def down_copy():
+        return rdma(
+            hsend.at[0],
+            gx.at[own, pl.ds(rows + halo, halo)],
+            z_send.at[0],
+            z_recv.at[0],
+            {"space": z - 1},
+        )
+
+    for i in range(n_own):
+        b_copy(i).start()
+    a_copy().start()
+
+    lanes = lax.broadcasted_iota(jnp.int32, (halo, tile), 1)
+    for side in range(2):
+        wanted = jnp.broadcast_to(send_ref[0, side : side + 1, :], (tile, halo)).T
+        picks = jnp.concatenate(
+            [(wanted == lanes + k * tile).astype(f32).astype(bf16) for k in range(rows // tile)],
+            axis=1,
+        )
+        hsend[side] = jnp.dot(picks, x_ref[...], preferred_element_type=f32).astype(bf16)
+
+    @pl.when(has_up)
+    def _():
+        up_copy().start()
+
+    @pl.when(has_down)
+    def _():
+        down_copy().start()
+
+    @pl.when(jnp.logical_not(has_down))
+    def _():
+        gx[own, pl.ds(rows, halo)] = jnp.zeros((halo, cols), bf16)
+
+    @pl.when(jnp.logical_not(has_up))
+    def _():
+        gx[own, pl.ds(rows + halo, halo)] = jnp.zeros((halo, cols), bf16)
+
+    w_copies[0].wait()
+    w_copies[1].wait()
+    wvt[...] = wv[...].astype(f32).T.astype(bf16)
+    local.wait()
+    a_copy().wait_recv()
+
+    def full_rows(at):
+        return jnp.concatenate([gx[g, at] for g in range(groups)], axis=1).astype(f32)
+
+    def norm(v, which):
+        mean = jnp.mean(v, axis=-1, keepdims=True)
+        spread = jnp.mean(v * v, axis=-1, keepdims=True) - mean * mean
+        scaled = (v - mean) * lax.rsqrt(spread + NORM_EPS)
+        return scaled * gains_ref[which : which + 1, :] + shifts_ref[which : which + 1, :]
+
+    def project(i, keep):
+        at = pl.ds(pl.multiple_of(i * chunk, chunk), chunk)
+        normed = norm(full_rows(at), 0).astype(bf16)
+        if keep:
+            nbuf[at] = normed
+        keys = jnp.dot(normed, wk[...], preferred_element_type=f32).astype(bf16)
+        values = lax.dot_general(wvt[...], normed, NT, preferred_element_type=f32).astype(bf16)
+        for k in range(per):
+            kbuf[i * per + k] = keys[k * tile : (k + 1) * tile]
+            vbuf[i * per + k] = values[:, k * tile : (k + 1) * tile]
+
+    b_copy(0).wait_recv()
+    c_copy(0).start()
+
+    def own_step(i, carry):
+        b_copy(i).wait_recv()
+        c_copy(i).start()
+        c_copy(i - 1).wait_recv()
+        project(i - 1, True)
+        return carry
+
+    lax.fori_loop(1, n_own - 1, own_step, 0)
+
+    @pl.when(has_down)
+    def _():
+        up_copy().wait_recv()
+
+    @pl.when(has_up)
+    def _():
+        down_copy().wait_recv()
+
+    b2_copy().start()
+    a2_copy().start()
+    lax.fori_loop(n_own - 1, n_own, own_step, 0)
+    c_copy(n_own - 1).wait_recv()
+    project(n_own - 1, True)
+
+    w_copies[2].wait()
+    own_at = pl.ds(pl.multiple_of(s * half_rows, half_rows), half_rows)
+    qbuf[...] = jnp.dot(nbuf[own_at], wq[...], preferred_element_type=f32).astype(bf16)
+    b2_copy().wait_recv()
+    c2_copy().start()
+    a2_copy().wait_recv()
+    c2_copy().wait_recv()
+
+    def halo_step(i, carry):
+        project(i, False)
+        return carry
+
+    lax.fori_loop(n_own, n_own + n_halo, halo_step, 0)
+
+    live = live_ref[0]
+    word_rows = tile // words
+    row_id = lax.broadcasted_iota(jnp.int32, (tile, tile), 0)
+    col_id = lax.broadcasted_iota(jnp.int32, (tile, tile), 1)
+    shifts = lax.broadcasted_iota(jnp.int32, (word_rows, tile), 0)
+    low_half = lax.broadcasted_iota(jnp.int32, (tile, pw), 1) < HD
+    scale = LOG2E / math.sqrt(HD)
+
+    def t_copy(j):
+        at = pl.ds(j * tile, tile)
+        return rdma(att.at[c, at], att.at[c, at], t_send.at[j], t_recv.at[j], xdev)
+
+    def attend_block(j, carry):
+        b = s * blocks_here + j
+        ids = [tk_ref[b, t] for t in range(slots)]
+        for t in range(slots):
+            block_bits = bits_ref[b, t]
+            set_bits = jnp.concatenate(
+                [
+                    jnp.right_shift(
+                        jnp.broadcast_to(block_bits[w : w + 1, :], (word_rows, tile)), shifts
+                    )
+                    & 1
+                    for w in range(words)
+                ],
+                axis=0,
+            )
+            limit = jnp.where(ids[t] >= blocks_own, tile, live - ids[t] * tile)
+            good = row_id < limit
+            if t == 0:
+                good = good | (row_id == col_id)
+            bias_ref[t * tile : (t + 1) * tile] = jnp.where(
+                (set_bits == 1) & good, 0.0, NEG_FILL
+            )
+        pieces = []
+        q_rows = qbuf[pl.ds(pl.multiple_of(j * tile, tile), tile)]
+        for pair in range(pairs):
+            at = slice(pair * pw, (pair + 1) * pw)
+            q_pair = q_rows[:, at]
+            zero = jnp.zeros_like(q_pair)
+            q_wide = jnp.concatenate(
+                [jnp.where(low_half, q_pair, zero), jnp.where(low_half, zero, q_pair)], axis=0
+            )
+            k_all = jnp.concatenate([kbuf[ids[t]][:, at] for t in range(slots)], axis=0)
+            scores = lax.dot_general(k_all, q_wide, NT, preferred_element_type=f32) * scale
+            bias = bias_ref[...]
+            scores = scores + jnp.concatenate([bias, bias], axis=1)
+            top = jnp.max(scores, axis=0, keepdims=True)
+            p = jnp.exp2(scores - top)
+            total = jnp.sum(p, axis=0, keepdims=True)
+            v_all = jnp.concatenate([vbuf[ids[t]][at, :] for t in range(slots)], axis=1)
+            mixed = jnp.dot(v_all, p.astype(bf16), preferred_element_type=f32) / total
+            pieces.append(mixed[:HD, :tile])
+            pieces.append(mixed[HD:, tile:])
+        att[c, pl.ds(pl.multiple_of(j * tile, tile), tile)] = (
+            jnp.concatenate(pieces, axis=0).T.astype(bf16)
+        )
+        t_copy(j).start()
+        return carry
+
+    lax.fori_loop(0, blocks_here, attend_block, 0)
+
+    for i in (3, 4, 5):
+        w_copies[i].wait()
+
+    n_ffn = half_rows // chunk
+
+    def p_copy(i):
+        at = pl.ds(i * chunk, chunk)
+        return rdma(psend.at[at], precv.at[at], p_send.at[i], p_recv.at[i], xdev)
+
+    def ffn_chunk(i, carry):
+        for k in range(per):
+            t_copy(i * per + k).wait_recv()
+        at = pl.ds(pl.multiple_of(i * chunk, chunk), chunk)
+        rows_at = pl.ds(pl.multiple_of(s * half_rows + i * chunk, chunk), chunk)
+        mixed = jnp.concatenate([att[g, at] for g in range(groups // 2)], axis=1)
+        after = full_rows(rows_at) + jnp.dot(mixed, wo[...], preferred_element_type=f32)
+        normed_two = norm(after, 1).astype(bf16)
+        hidden = gelu_tanh(
+            lax.dot_general(normed_two, fin[...], NT, preferred_element_type=f32)
+        ).astype(bf16)
+        part = jnp.dot(hidden, fout[...], preferred_element_type=f32)
+        left, right = part[:, :head_cols], part[:, head_cols:]
+        first = c == 0
+        psend[at] = jnp.where(first, right, left).astype(bf16)
+        p_copy(i).start()
+        own_part[at] = jnp.where(first, left + after[:, :head_cols], right + after[:, head_cols:])
+        return carry
+
+    lax.fori_loop(0, n_ffn, ffn_chunk, 0)
+
+    def o_copy(i):
+        at = pl.ds(i * chunk, chunk)
+        out_at = pl.ds(s * half_rows + i * chunk, chunk)
+        return rdma(osend.at[at], out_ref.at[out_at], o_send.at[i], o_recv.at[i], sdev)
+
+    def finish(i, carry):
+        p_copy(i).wait_recv()
+        at = pl.ds(pl.multiple_of(i * chunk, chunk), chunk)
+        base = s * half_rows + i * chunk
+        summed = own_part[at] + precv[at].astype(f32)
+        position = base + lax.broadcasted_iota(jnp.int32, (chunk, head_cols), 0)
+        done = jnp.where(position < live, summed, 0.0)
+        left, right = done[:, :cols], done[:, cols:]
+        first = s == 0
+        osend[at] = jnp.where(first, right, left).astype(bf16)
+        o_copy(i).start()
+        out_ref[pl.ds(pl.multiple_of(base, chunk), chunk)] = jnp.where(
+            first, left, right
+        ).astype(bf16)
+        return carry
+
+    lax.fori_loop(0, n_ffn, finish, 0)
+
+    a_copy().wait_send()
+    a2_copy().wait_send()
+    b2_copy().wait_send()
+    c2_copy().wait_send()
+    for i in range(n_own):
+        b_copy(i).wait_send()
+        c_copy(i).wait_send()
+    for j in range(blocks_here):
+        t_copy(j).wait_send()
+
+    @pl.when(has_up)
+    def _():
+        up_copy().wait_send()
+
+    @pl.when(has_down)
+    def _():
+        down_copy().wait_send()
+
+    for i in range(n_ffn):
+        p_copy(i).wait_send()
+        o_copy(i).wait()
+
+
+def one_kernel(*args):
+    (x, gains, shifts, wq, wk, wv, wo, fin, fout, live, send, tk, bits) = args
+    bf16 = jnp.bfloat16
+    rows, cols = x.shape
+    width = gains.shape[1]
+    groups = lax.axis_size("chan") * lax.axis_size("sub")
+    halo = send.shape[-1]
+    tile = bits.shape[-1]
+    slots = tk.shape[1]
+    ext = rows + 2 * halo
+    head_cols = wq.shape[1]
+    half = rows // 2
+    chunk = 2 * tile
+    n_own = rows // chunk
+    blocks_here = tk.shape[0] // 2
+    n_ffn = half // chunk
+    vmem = pltpu.VMEM
+    dma = pltpu.SemaphoreType.DMA
+    in_vmem = pl.BlockSpec(memory_space=pltpu.VMEM)
+    in_smem = pl.BlockSpec(memory_space=pltpu.SMEM)
+    in_any = pl.BlockSpec(memory_space=pl.ANY)
+    return pl.pallas_call(
+        layer_kernel,
+        out_shape=jax.ShapeDtypeStruct(x.shape, bf16),
+        in_specs=[in_vmem] * 3 + [in_any] * 6 + [in_smem, in_vmem, in_smem, in_vmem],
+        out_specs=in_vmem,
+        scratch_shapes=[
+            vmem((groups, ext, cols), bf16),
+            vmem((2, halo, cols), bf16),
+            vmem((rows, width), bf16),
+            vmem((ext // tile, tile, head_cols), bf16),
+            vmem((ext // tile, head_cols, tile), bf16),
+            vmem((head_cols, width), bf16),
+            vmem((half, head_cols), bf16),
+            vmem((slots * tile, tile), jnp.float32),
+            vmem((2, half, head_cols), bf16),
+            vmem((half, head_cols), jnp.float32),
+            vmem((half, head_cols), bf16),
+            vmem((half, head_cols), bf16),
+            vmem((half, cols), bf16),
+            vmem(wq.shape, bf16),
+            vmem(wk.shape, bf16),
+            vmem(wv.shape, bf16),
+            vmem(wo.shape, bf16),
+            vmem(fin.shape, bf16),
+            vmem(fout.shape, bf16),
+            dma((6,)),
+            dma,
+            dma((2,)),
+            dma((2,)),
+            dma((n_own + 1,)),
+            dma((n_own + 1,)),
+            dma((n_own + 1,)),
+            dma((n_own + 1,)),
+            dma((2,)),
+            dma((2,)),
+            dma((blocks_here,)),
+            dma((blocks_here,)),
+            dma((n_ffn,)),
+            dma((n_ffn,)),
+            dma((n_ffn,)),
+            dma((n_ffn,)),
+        ],
+        compiler_params=pltpu.CompilerParams(collective_id=0, has_side_effects=True),
+    )(*args)
+
+
+def on_any_device(*args):
+    two_by_two = lax.axis_size("chan") == 2 and lax.axis_size("sub") == 2
+    cols, head_cols = args[0].shape[1], args[3].shape[1]
+    tile, halo = args[12].shape[-1], args[10].shape[-1]
+    rows_fit = args[0].shape[0] % (4 * tile) == 0 and 2 * halo % (2 * tile) == 0
+    if two_by_two and cols % 128 == 0 and head_cols % (2 * HD) == 0 and rows_fit:
+        return one_kernel(*args)
+    return on_device(*args)
+
+
 def solution(mesh):
     in_specs = (
         P(("ens", "space"), ("chan", "sub")),
@@ -201,5 +667,5 @@
     )
     out_specs = P(("ens", "space"), ("chan", "sub"))
     return jax.shard_map(
-        on_device, mesh=mesh, in_specs=in_specs, out_specs=out_specs, check_vma=False
-    )
+        on_any_device, mesh=mesh, in_specs=in_specs, out_specs=out_specs, check_vma=False
+    )

time: 128 us -> 40.3 us (0.31)
  Pallas kernels: 0 us -> 37.8 us
  waiting for transfers between devices: 30.2 us -> 0 us
  local copies, waits for them, and re-layouts: 28.3 us -> 1.67 us
  blocking collectives: 23 us -> 0 us
  between operations: 14.3 us -> 0.66 us
  matrix products: 11.2 us -> 0 us
  other arithmetic: 11.2 us -> 0 us
  starting transfers between devices: 8.95 us -> 0 us
    pallas_call x0 -> x1, Pallas kernels: none -> 37.8 us  [one_kernel(): pl.pallas_call(layer_kernel, out_shape=jax.ShapeDtypeStruct(x.shape, bf16...]
    all_to_all x2 -> x0, blocking collectives: 16 us -> none  [the longest x1 8.39 us: on_device(): lax.all_to_all(result, ('chan', 'sub'), split_axis=1, concat_axis=0, tile...]
    gather x3 -> x0, local copies, waits for them, and re-layouts: 15.6 us -> none  [the longest x2 13.6 us: attend(): chosen = key_blocks[id_part]]
    reduce_scatter x1 -> x0, waiting for transfers between devices: 13.8 us -> none  [on_device(): lax.psum_scatter(hidden_term(all_rows, ffn_in, ffn_out).astype(jnp.bfloat...]
    dot_general x6 -> x0, matrix products: 11.2 us -> none  [the longest x1 3.42 us: attend(): jnp.einsum('ghrtk,gtkhd->grhd', weights.astype(jnp.bfloat16), values_part...]
    all_gather x1 -> x0, waiting for transfers between devices: 10 us -> none  [on_device(): gathered = lax.all_gather(node_state, ('chan', 'sub'), axis=1, tiled=True)]
    all_gather x1 -> x0, blocking collectives: 7.04 us -> none  [on_device(): all_rows = lax.all_gather(normed_two, 'chan', axis=0, tiled=True)]
    ppermute x2 -> x0, waiting for transfers between devices: 5.7 us -> none  [the longest x1 3.53 us: padded_2(): after = lax.ppermute(leading, axis, down)]
  transfers between devices with their start and end apart: 5 -> 0, of which waited for: 4 -> 0; matrix products, arithmetic and copies ran while one was open for 34% -> 0% of each run, Pallas kernels for 0% -> 0%
where the time goes in v1:
time: 40.3 us; the launch traced here: 40.2 us
  Pallas kernels  37.8 us (94%)
  local copies, waits for them, and re-layouts  1.67 us (4%)
  between operations  0.66 us (2%)
    pallas_call x1, Pallas kernels, one_kernel(): pl.pallas_call(layer_kernel, out_shape=jax.ShapeDtypeStruct(x.shape, bf16...  37.8 us
    unnamed x1, local copies, waits for them, and re-layouts  1.67 us

profile of v1, /device:TPU:0, one launch (start us, length us, event | category | flops | bytes accessed | tf_op | source)
XLA Modules:
  0.0 40.2 jit_solution(14077266522739325844)
XLA Ops:
  0.7 37.8 %shard_map.127 = bf16[1024,128]{1,0:T(8,128)(2,1)} custom-call(bf16[1024,128]{1,0:T(8,128)(2,1)} %x_ref.1, f32[2,512]{1,0:T(2,128)} %gains_ref.1, f32[2,512]{1,0:T(2,128)} %shifts_ref.1, bf16[512,256]{1,0:T(8,128)(2,1)} %wq_hbm.1, bf16[512,256]{1,0:T(8,128)(2,1)} %wk_hbm.1, bf16[512,256]{1,0:T(8,128)(2,1)} %wv_hbm.1, bf16[512,512]{1,0:T(8,128)(2,1)} %wo_hbm.1, ...), custom_call_target="tpu_custom_call" | custom-call | tf_op jit(solution)/shard_map/pallas_call | solution.py:596
  38.5 1.7 %copy.16 = bf16[1024,128]{1,0:T(8,128)(2,1)} copy(bf16[1024,128]{1,0:T(8,128)(2,1)} %shard_map.127) | data formatting | bytes 524288

commit v2 on v1

--- a/solution.py
+++ b/solution.py
@@ -196,9 +196,9 @@
 
 
 def layer_kernel(
-    x_ref,
-    gains_ref,
-    shifts_ref,
+    x_hbm,
+    gains_hbm,
+    shifts_hbm,
     wq_hbm,
     wk_hbm,
     wv_hbm,
@@ -206,9 +206,9 @@
     fin_hbm,
     fout_hbm,
     live_ref,
-    send_ref,
+    send_hbm,
     tk_ref,
-    bits_ref,
+    bits_hbm,
     out_ref,
     gx,
     hsend,
@@ -217,7 +217,7 @@
     vbuf,
     wvt,
     qbuf,
-    bias_ref,
+    s_ref,
     att,
     own_part,
     psend,
@@ -229,6 +229,10 @@
     wo,
     fin,
     fout,
+    gains_ref,
+    shifts_ref,
+    send_ref,
+    bits_ref,
     w_sem,
     loc_sem,
     a_send,
@@ -247,13 +251,13 @@
     o_recv,
 ):
     f32, bf16 = jnp.float32, jnp.bfloat16
-    rows, cols = x_ref.shape
+    rows, cols = x_hbm.shape
     groups, ext_rows, _ = gx.shape
-    tile = bits_ref.shape[-1]
-    words = bits_ref.shape[-2]
+    tile = bits_hbm.shape[-1]
+    words = bits_hbm.shape[-2]
     slots = tk_ref.shape[1]
     blocks_own = tk_ref.shape[0]
-    halo = send_ref.shape[-1]
+    halo = send_hbm.shape[-1]
     head_cols = wq.shape[1]
     pairs = head_cols // (2 * HD)
     pw = 2 * HD
@@ -275,12 +279,21 @@
     has_up = z < nz - 1
     has_down = z > 0
 
-    weights = ((wk_hbm, wk), (wv_hbm, wv), (wq_hbm, wq), (wo_hbm, wo), (fin_hbm, fin), (fout_hbm, fout))
-    w_copies = [pltpu.make_async_copy(a, b, w_sem.at[i]) for i, (a, b) in enumerate(weights)]
-    for w_copy in w_copies:
-        w_copy.start()
-    local = pltpu.make_async_copy(x_ref, gx.at[own, pl.ds(0, rows)], loc_sem)
+    local = pltpu.make_async_copy(x_hbm, gx.at[own, pl.ds(0, rows)], loc_sem)
     local.start()
+    loads = (
+        (send_hbm, send_ref),
+        (wv_hbm, wv),
+        (gains_hbm, gains_ref),
+        (shifts_hbm, shifts_ref),
+        (wk_hbm, wk),
+        (wq_hbm, wq),
+        (bits_hbm, bits_ref),
+        (wo_hbm, wo),
+        (fin_hbm, fin),
+        (fout_hbm, fout),
+    )
+    w_copies = [pltpu.make_async_copy(a, b, w_sem.at[i]) for i, (a, b) in enumerate(loads)]
 
     barrier = pltpu.get_barrier_semaphore()
     pl.semaphore_signal(barrier, inc=1, device_id=xdev, device_id_type=MESH)
@@ -294,6 +307,8 @@
     def _():
         pl.semaphore_signal(barrier, inc=1, device_id={"space": z - 1}, device_id_type=MESH)
 
+    for w_copy in w_copies:
+        w_copy.start()
     pl.semaphore_wait(barrier, 2 + jnp.where(has_up, 1, 0) + jnp.where(has_down, 1, 0))
 
     def rdma(src, dst, ss, rs, dev):
@@ -302,11 +317,11 @@
         )
 
     def a_copy():
-        return rdma(x_ref, gx.at[own, pl.ds(0, rows)], a_send.at[0], a_recv.at[0], sdev)
+        return rdma(gx.at[own, pl.ds(0, rows)], gx.at[own, pl.ds(0, rows)], a_send.at[0], a_recv.at[0], sdev)
 
     def b_copy(i):
         at = pl.ds(i * chunk, chunk)
-        return rdma(x_ref.at[at], gx.at[own, at], b_send.at[i], b_recv.at[i], xdev)
+        return rdma(gx.at[own, at], gx.at[own, at], b_send.at[i], b_recv.at[i], xdev)
 
     def c_copy(i):
         at = pl.ds(i * chunk, chunk)
@@ -339,9 +354,11 @@
             {"space": z - 1},
         )
 
+    local.wait()
     for i in range(n_own):
         b_copy(i).start()
     a_copy().start()
+    w_copies[0].wait()
 
     lanes = lax.broadcasted_iota(jnp.int32, (halo, tile), 1)
     for side in range(2):
@@ -350,7 +367,7 @@
             [(wanted == lanes + k * tile).astype(f32).astype(bf16) for k in range(rows // tile)],
             axis=1,
         )
-        hsend[side] = jnp.dot(picks, x_ref[...], preferred_element_type=f32).astype(bf16)
+        hsend[side] = jnp.dot(picks, gx[own, pl.ds(0, rows)], preferred_element_type=f32).astype(bf16)
 
     @pl.when(has_up)
     def _():
@@ -368,10 +385,9 @@
     def _():
         gx[own, pl.ds(rows + halo, halo)] = jnp.zeros((halo, cols), bf16)
 
-    w_copies[0].wait()
-    w_copies[1].wait()
+    for i in range(1, 5):
+        w_copies[i].wait()
     wvt[...] = wv[...].astype(f32).T.astype(bf16)
-    local.wait()
     a_copy().wait_recv()
 
     def full_rows(at):
@@ -420,9 +436,12 @@
     c_copy(n_own - 1).wait_recv()
     project(n_own - 1, True)
 
-    w_copies[2].wait()
+    scale = LOG2E / math.sqrt(HD)
+    w_copies[5].wait()
     own_at = pl.ds(pl.multiple_of(s * half_rows, half_rows), half_rows)
-    qbuf[...] = jnp.dot(nbuf[own_at], wq[...], preferred_element_type=f32).astype(bf16)
+    q_rows = jnp.dot(nbuf[own_at], wq[...], preferred_element_type=f32) * scale
+    qbuf[...] = q_rows.astype(bf16)
+    w_copies[6].wait()
     b2_copy().wait_recv()
     c2_copy().start()
     a2_copy().wait_recv()
@@ -440,15 +459,27 @@
     col_id = lax.broadcasted_iota(jnp.int32, (tile, tile), 1)
     shifts = lax.broadcasted_iota(jnp.int32, (word_rows, tile), 0)
     low_half = lax.broadcasted_iota(jnp.int32, (tile, pw), 1) < HD
-    scale = LOG2E / math.sqrt(HD)
 
     def t_copy(j):
         at = pl.ds(j * tile, tile)
         return rdma(att.at[c, at], att.at[c, at], t_send.at[j], t_recv.at[j], xdev)
 
+    ones = jnp.ones((16, 2 * tile), bf16)
+
     def attend_block(j, carry):
         b = s * blocks_here + j
         ids = [tk_ref[b, t] for t in range(slots)]
+        q_rows = qbuf[pl.ds(pl.multiple_of(j * tile, tile), tile)]
+        wide = []
+        for pair in range(pairs):
+            q_pair = q_rows[:, pair * pw : (pair + 1) * pw]
+            zero = jnp.zeros_like(q_pair)
+            wide.append(
+                jnp.concatenate(
+                    [jnp.where(low_half, q_pair, zero), jnp.where(low_half, zero, q_pair)], axis=0
+                )
+            )
+        tops = [jnp.full((8, 2 * tile), NEG_FILL, f32) for _ in range(pairs)]
         for t in range(slots):
             block_bits = bits_ref[b, t]
             set_bits = jnp.concatenate(
@@ -465,29 +496,28 @@
             good = row_id < limit
             if t == 0:
                 good = good | (row_id == col_id)
-            bias_ref[t * tile : (t + 1) * tile] = jnp.where(
-                (set_bits == 1) & good, 0.0, NEG_FILL
-            )
+            bias = jnp.where((set_bits == 1) & good, 0.0, NEG_FILL)
+            bias = jnp.concatenate([bias, bias], axis=1)
+            for pair in range(pairs):
+                keys = kbuf[ids[t], :, pair * pw : (pair + 1) * pw]
+                scores = lax.dot_general(keys, wide[pair], NT, preferred_element_type=f32) + bias
+                s_ref[pair, t * tile : (t + 1) * tile] = scores
+                tops[pair] = jnp.maximum(
+                    tops[pair], jnp.max(scores.reshape(tile // 8, 8, 2 * tile), axis=0)
+                )
         pieces = []
-        q_rows = qbuf[pl.ds(pl.multiple_of(j * tile, tile), tile)]
         for pair in range(pairs):
-            at = slice(pair * pw, (pair + 1) * pw)
-            q_pair = q_rows[:, at]
-            zero = jnp.zeros_like(q_pair)
-            q_wide = jnp.concatenate(
-                [jnp.where(low_half, q_pair, zero), jnp.where(low_half, zero, q_pair)], axis=0
-            )
-            k_all = jnp.concatenate([kbuf[ids[t]][:, at] for t in range(slots)], axis=0)
-            scores = lax.dot_general(k_all, q_wide, NT, preferred_element_type=f32) * scale
-            bias = bias_ref[...]
-            scores = scores + jnp.concatenate([bias, bias], axis=1)
-            top = jnp.max(scores, axis=0, keepdims=True)
-            p = jnp.exp2(scores - top)
-            total = jnp.sum(p, axis=0, keepdims=True)
-            v_all = jnp.concatenate([vbuf[ids[t]][at, :] for t in range(slots)], axis=1)
-            mixed = jnp.dot(v_all, p.astype(bf16), preferred_element_type=f32) / total
-            pieces.append(mixed[:HD, :tile])
-            pieces.append(mixed[HD:, tile:])
+            top = jnp.max(tops[pair], axis=0, keepdims=True)
+            mixed = jnp.zeros((pw + 16, 2 * tile), f32)
+            for t in range(0, slots, 2):
+                p = jnp.exp2(s_ref[pair, t * tile : (t + 2) * tile] - top).astype(bf16)
+                at = slice(pair * pw, (pair + 1) * pw)
+                values = jnp.concatenate([vbuf[ids[t], at], vbuf[ids[t + 1], at]], axis=1)
+                values = jnp.concatenate([values, ones], axis=0)
+                mixed = mixed + jnp.dot(values, p, preferred_element_type=f32)
+            inverse = 1.0 / mixed[pw : pw + 1]
+            pieces.append(mixed[:HD, :tile] * inverse[:, :tile])
+            pieces.append(mixed[HD:pw, tile:] * inverse[:, tile:])
         att[c, pl.ds(pl.multiple_of(j * tile, tile), tile)] = (
             jnp.concatenate(pieces, axis=0).T.astype(bf16)
         )
@@ -496,7 +526,7 @@
 
     lax.fori_loop(0, blocks_here, attend_block, 0)
 
-    for i in (3, 4, 5):
+    for i in (7, 8, 9):
         w_copies[i].wait()
 
     n_ffn = half_rows // chunk
@@ -596,7 +626,7 @@
     return pl.pallas_call(
         layer_kernel,
         out_shape=jax.ShapeDtypeStruct(x.shape, bf16),
-        in_specs=[in_vmem] * 3 + [in_any] * 6 + [in_smem, in_vmem, in_smem, in_vmem],
+        in_specs=[in_any] * 9 + [in_smem, in_any, in_smem, in_any],
         out_specs=in_vmem,
         scratch_shapes=[
             vmem((groups, ext, cols), bf16),
@@ -606,7 +636,7 @@
             vmem((ext // tile, head_cols, tile), bf16),
             vmem((head_cols, width), bf16),
             vmem((half, head_cols), bf16),
-            vmem((slots * tile, tile), jnp.float32),
+            vmem((head_cols // (2 * HD), slots * tile, 2 * tile), jnp.float32),
             vmem((2, half, head_cols), bf16),
             vmem((half, head_cols), jnp.float32),
             vmem((half, head_cols), bf16),
@@ -618,7 +648,11 @@
             vmem(wo.shape, bf16),
             vmem(fin.shape, bf16),
             vmem(fout.shape, bf16),
-            dma((6,)),
+            vmem(gains.shape, jnp.float32),
+            vmem(shifts.shape, jnp.float32),
+            vmem(send.shape, jnp.int32),
+            vmem(bits.shape, jnp.int32),
+            dma((10,)),
             dma,
             dma((2,)),
             dma((2,)),
@@ -644,7 +678,7 @@
     cols, head_cols = args[0].shape[1], args[3].shape[1]
     tile, halo = args[12].shape[-1], args[10].shape[-1]
     rows_fit = args[0].shape[0] % (4 * tile) == 0 and 2 * halo % (2 * tile) == 0
-    if two_by_two and cols % 128 == 0 and head_cols % (2 * HD) == 0 and rows_fit:
+    if two_by_two and cols % 128 == 0 and head_cols % (2 * HD) == 0 and rows_fit and args[11].shape[1] % 2 == 0:
         return one_kernel(*args)
     return on_device(*args)
 

time: 40.3 us -> 37.3 us (0.926)
  Pallas kernels: 37.8 us -> 34.8 us
    pallas_call x1, Pallas kernels: 37.8 us -> 34.8 us  [one_kernel(): pl.pallas_call(layer_kernel, out_shape=jax.ShapeDtypeStruct(x.shape, bf16...]
where the time goes in v2:
time: 37.3 us; the launch traced here: 37.1 us
  Pallas kernels  34.8 us (93%)
  local copies, waits for them, and re-layouts  1.67 us (4%)
  between operations  0.66 us (2%)
    pallas_call x1, Pallas kernels, one_kernel(): pl.pallas_call(layer_kernel, out_shape=jax.ShapeDtypeStruct(x.shape, bf16...  34.8 us
    unnamed x1, local copies, waits for them, and re-layouts  1.67 us

profile of v2, /device:TPU:0, one launch (start us, length us, event | category | flops | bytes accessed | tf_op | source)
XLA Modules:
  0.0 37.1 jit_solution(3844501946873703607)
XLA Ops:
  0.7 34.8 %shard_map.127 = bf16[1024,128]{1,0:T(8,128)(2,1)} custom-call(bf16[1024,128]{1,0:T(8,128)(2,1)} %x_hbm.1, f32[2,512]{1,0:T(2,128)} %gains_hbm.1, f32[2,512]{1,0:T(2,128)} %shifts_hbm.1, bf16[512,256]{1,0:T(8,128)(2,1)} %wq_hbm.1, bf16[512,256]{1,0:T(8,128)(2,1)} %wk_hbm.1, bf16[512,256]{1,0:T(8,128)(2,1)} %wv_hbm.1, bf16[512,512]{1,0:T(8,128)(2,1)} %wo_hbm.1, ...), custom_call_target="tpu_custom_call" | custom-call | tf_op jit(solution)/shard_map/pallas_call | solution.py:626
  35.4 1.7 %copy.16 = bf16[1024,128]{1,0:T(8,128)(2,1)} copy(bf16[1024,128]{1,0:T(8,128)(2,1)} %shard_map.127) | data formatting | bytes 524288

commit v3 on v2

--- a/solution.py
+++ b/solution.py
@@ -625,7 +625,7 @@
     in_any = pl.BlockSpec(memory_space=pl.ANY)
     return pl.pallas_call(
         layer_kernel,
-        out_shape=jax.ShapeDtypeStruct(x.shape, bf16),
+        out_shape=pltpu.VMEM(x.shape, bf16),
         in_specs=[in_any] * 9 + [in_smem, in_any, in_smem, in_any],
         out_specs=in_vmem,
         scratch_shapes=[

time: 37.3 us -> 35.6 us (0.954)
  local copies, waits for them, and re-layouts: 1.67 us -> 0.71 us
  Pallas kernels: 34.8 us -> 34.1 us
    unnamed x1, local copies, waits for them, and re-layouts: 1.67 us -> 0.71 us
    pallas_call x1, Pallas kernels: 34.8 us -> 34.1 us  [one_kernel(): pl.pallas_call(layer_kernel, out_shape=pltpu.VMEM(x.shape, bf16), in_spec...]
where the time goes in v3:
time: 35.6 us; the launch traced here: 35.5 us
  Pallas kernels  34.1 us (96%)
  local copies, waits for them, and re-layouts  0.71 us (2%)
  between operations  0.66 us (2%)
    pallas_call x1, Pallas kernels, one_kernel(): pl.pallas_call(layer_kernel, out_shape=pltpu.VMEM(x.shape, bf16), in_spec...  34.1 us

profile of v3, /device:TPU:0, one launch (start us, length us, event | category | flops | bytes accessed | tf_op | source)
XLA Modules:
  0.0 35.5 jit_solution(6095529625187853362)
XLA Ops:
  0.7 34.1 %shard_map.127 = bf16[1024,128]{1,0:T(8,128)(2,1)S(1)} custom-call(bf16[1024,128]{1,0:T(8,128)(2,1)} %x_hbm.1, f32[2,512]{1,0:T(2,128)} %gains_hbm.1, f32[2,512]{1,0:T(2,128)} %shifts_hbm.1, bf16[512,256]{1,0:T(8,128)(2,1)} %wq_hbm.1, bf16[512,256]{1,0:T(8,128)(2,1)} %wk_hbm.1, bf16[512,256]{1,0:T(8,128)(2,1)} %wv_hbm.1, bf16[512,512]{1,0:T(8,128)(2,1)} %wo_hbm.1, ...), custom_call_target="tpu_custom_call" | custom-call | tf_op jit(solution)/shard_map/pallas_call | solution.py:626
  34.8 0.7 %copy.15 = bf16[1024,128]{1,0:T(8,128)(2,1)} copy(bf16[1024,128]{1,0:T(8,128)(2,1)S(1)} %shard_map.127) | data formatting | bytes 524288
